TPU v7x, 32 devices: a whole 2x2x4 slice. The times are simulated.
32 devices in a mesh: groups: 2 (over y), seq: 4 (over z), heads: 2 (over x), cfg: 2 (over core).
Axes of the slice: x: 2, y: 2, z: 4, core: 2. Of those that a mesh axis runs over, the one named last changes fastest.
Arguments:
- video_tokens: bfloat16 [2, 8, 1152, 1024], P('cfg', ('groups', 'seq'), 'heads'), parts along dimension 1, may hold values from -6 to 6
- text_tokens: bfloat16 [2, 8, 1152, 128], P('cfg', ('groups', 'seq'), 'heads'), parts along dimension 1, may hold values from -6 to 6
- text_length: int32 [2, 8], P('cfg', ('groups', 'seq')), parts along dimension 1, may hold values from 1 to 128
- guide_numer: int32 [8], P(('groups', 'seq')), parts along dimension 0, may hold values from 2 to 8
- guide_denom: int32 [8], P(('groups', 'seq')), parts along dimension 0, may hold values from 4 to 8
- spatial_gain: bfloat16 [1152], replicated, may hold values from 0.25 to 1.75
- spatial_qkv: bfloat16 [3, 1152, 1152], P(None, 'heads'), may hold values from -0.11785113 to 0.11785113
- spatial_out: bfloat16 [1152, 1152], P('heads'), may hold values from -0.1875 to 0.1875
- temporal_gain: bfloat16 [1152], replicated, may hold values from 0.25 to 1.75
- temporal_qkv: bfloat16 [3, 1152, 1152], P(None, 'heads'), may hold values from -0.11785113 to 0.11785113
- temporal_out: bfloat16 [1152, 1152], P('heads'), may hold values from -0.1875 to 0.1875
Outputs:
- guided: bfloat16 [8, 1152, 1024], P(('groups', 'seq'), ('heads', 'cfg')), parts along dimension 0
There are 2 independent parts, one for each index of `groups`. A program takes and returns all parts, laid end to end along the dimension named above; an argument that names none is the same for every part. Nothing has to cross between parts.
Inputs may be any that keep to these rules, and one draw needn't show every extreme that they name: `text_length`: text tokens at or beyond a frame's length are padding.
All inputs are finite; a program needn't handle non-finite values.
Results may differ from a plain program's by a relative error of at most 0.009.
Values may be sent and summed in bfloat16 or wider, within the bound.
A program may use at most 64 MiB of HBM per device.

v0:
```python
import jax
import jax.numpy as jnp
from jax import lax
from jax.sharding import PartitionSpec as P

D = 1152
HEAD_DIM = 72
epsilon = 1e-06


def from_partner(shard, axis, stride):
    return lax.ppermute(shard, axis, [(i, i ^ 1 << stride) for i in range(lax.axis_size(axis))])


def softmax_along(scores, axis):
    top_score = jnp.max(scores, axis=axis, keepdims=True)
    expons = jnp.exp(scores - top_score)
    return (expons / jnp.sum(expons, axis=axis, keepdims=True)).astype(jnp.bfloat16)


def project_piece(piece, gain_vector, weights, parts):
    gain_piece = gain_vector.astype(jnp.float32)
    weight_piece = weights[parts]
    piece_wide = piece.astype(jnp.float32)
    scaled = (piece_wide * gain_piece[None, :, None]).astype(jnp.bfloat16)
    product = jnp.einsum("kod,fdp->fkop", weight_piece, scaled, preferred_element_type=jnp.float32)
    return (product, jnp.sum(piece_wide * piece_wide, axis=1))


def add_mixed(piece, matrix):
    return jnp.einsum("oc,fcp->fop", matrix, piece, preferred_element_type=jnp.float32)


def shards(
    video_tokens,
    text_tokens,
    text_length,
    guide_numer,
    guide_denom,
    spatial_gain,
    spatial_qkv,
    spatial_out,
    temporal_gain,
    temporal_qkv,
    temporal_out,
):
    frame_count = video_tokens.shape[1]
    width = video_tokens.shape[2]
    positions = video_tokens.shape[3]
    text_count = text_tokens.shape[3]
    local_heads = width // HEAD_DIM
    frame_tokens = video_tokens[0]
    frame_text = text_tokens[0]
    video_piece = lax.all_gather(frame_tokens, "heads", axis=1, tiled=True)
    text_piece = lax.all_gather(frame_text, "heads", axis=1, tiled=True)
    video_add, video_sq = project_piece(video_piece, spatial_gain, spatial_qkv, slice(0, 3))
    text_add, text_sq = project_piece(text_piece, spatial_gain, spatial_qkv, slice(1, 3))
    mixed = (video_add * lax.rsqrt(video_sq / D + epsilon)[:, None, None, :]).astype(jnp.bfloat16)
    mixed = mixed.reshape(frame_count, 3, local_heads, HEAD_DIM, positions)
    context = (text_add * lax.rsqrt(text_sq / D + epsilon)[:, None, None, :]).astype(jnp.bfloat16)
    context = context.reshape(frame_count, 2, local_heads, HEAD_DIM, text_count)
    key_rows = jnp.concatenate([mixed[:, 1], context[:, 0]], axis=3)
    value_rows = jnp.concatenate([mixed[:, 2], context[:, 1]], axis=3)
    query_all = mixed[:, 0]
    text_valid = jnp.arange(text_count, dtype=jnp.int32)[None, :] < text_length[0][:, None]
    valid_keys = jnp.concatenate(
        [jnp.ones((frame_count, positions), dtype=bool), text_valid], axis=1
    )
    block_rows = min(512, positions)
    block_count = positions // block_rows
    frame_ids = jnp.repeat(jnp.arange(frame_count, dtype=jnp.int32), block_count)
    block_ids = jnp.tile(jnp.arange(block_count, dtype=jnp.int32), frame_count)

    def block_step(inputs):
        frame_id, block_id = inputs
        query_rows = lax.dynamic_slice_in_dim(
            query_all[frame_id], block_id * block_rows, block_rows, 2
        )
        scores = jnp.einsum(
            "hep,hek->hpk", query_rows, key_rows[frame_id], preferred_element_type=jnp.float32
        )
        scores = scores * HEAD_DIM ** (-0.5)
        scores = jnp.where(valid_keys[frame_id][None, None, :], scores, -jnp.inf)
        weights = softmax_along(scores, 2)
        result = jnp.einsum(
            "hpk,hek->hep", weights, value_rows[frame_id], preferred_element_type=jnp.float32
        )
        return result.astype(jnp.bfloat16)

    attended = lax.map(block_step, (frame_ids, block_ids))
    attended = attended.reshape(frame_count, block_count, local_heads, HEAD_DIM, block_rows)
    attended = jnp.transpose(attended, (0, 2, 3, 1, 4)).reshape(frame_count, width, positions)
    update = add_mixed(lax.all_gather(attended, "heads", axis=1, tiled=True), spatial_out)
    after_spatial = (frame_tokens.astype(jnp.float32) + update).astype(jnp.bfloat16)
    own_rows = lax.all_to_all(after_spatial, "seq", split_axis=2, concat_axis=0, tiled=True)
    frames_all = own_rows.shape[0]
    columns = own_rows.shape[2]
    piece_add, piece_sq = project_piece(
        lax.all_gather(own_rows, "heads", axis=1, tiled=True),
        temporal_gain,
        temporal_qkv,
        slice(0, 3),
    )
    mixed_time = (piece_add * lax.rsqrt(piece_sq / D + epsilon)[:, None, None, :]).astype(
        jnp.bfloat16
    )
    mixed_time = mixed_time.reshape(frames_all, 3, local_heads, HEAD_DIM, columns)
    time_scores = jnp.einsum(
        "fhep,ghep->hfgp", mixed_time[:, 0], mixed_time[:, 1], preferred_element_type=jnp.float32
    )
    time_weights = softmax_along(time_scores * HEAD_DIM ** (-0.5), 2)
    attended_time = jnp.einsum(
        "hfgp,ghep->fhep", time_weights, mixed_time[:, 2], preferred_element_type=jnp.float32
    )
    attended_time = attended_time.astype(jnp.bfloat16).reshape(frames_all, width, columns)
    update_time = add_mixed(
        lax.all_gather(attended_time, "heads", axis=1, tiled=True), temporal_out
    )
    block_out = (own_rows.astype(jnp.float32) + update_time).astype(jnp.bfloat16)
    returned = lax.all_to_all(block_out, "seq", split_axis=0, concat_axis=2, tiled=True)
    half_width = width // 2
    partner = from_partner(returned, "cfg", 0)
    branch_index = lax.axis_index("cfg")
    cond_full = jnp.where(branch_index == 0, returned, partner)
    uncond_full = jnp.where(branch_index == 0, partner, returned)
    cond_part = lax.dynamic_slice_in_dim(cond_full, branch_index * half_width, half_width, 1)
    uncond_part = lax.dynamic_slice_in_dim(uncond_full, branch_index * half_width, half_width, 1)
    ratio = guide_numer.astype(jnp.float32) / guide_denom.astype(jnp.float32)
    cond_wide = cond_part.astype(jnp.float32)
    uncond_wide = uncond_part.astype(jnp.float32)
    return (uncond_wide + ratio[:, None, None] * (cond_wide - uncond_wide)).astype(jnp.bfloat16)


def solution(mesh):
    return jax.shard_map(
        shards,
        mesh=mesh,
        in_specs=(
            P("cfg", ("groups", "seq"), "heads", None),
            P("cfg", ("groups", "seq"), "heads", None),
            P("cfg", ("groups", "seq")),
            P(("groups", "seq")),
            P(("groups", "seq")),
            P(),
            P(None, "heads", None),
            P("heads", None),
            P(),
            P(None, "heads", None),
            P("heads", None),
        ),
        out_specs=P(("groups", "seq"), ("heads", "cfg"), None),
        check_vma=False,
    )
```

profile of v0, /device:TPU:0, one launch (start us, length us, event | category | flops | bytes accessed | tf_op | source)
XLA Modules:
  0.0 359.0 jit_solution(843548291912899709)
XLA Ops:
  8.7 7.7 %all-gather.1 = bf16[1,1,1152,128]{3,2,1,0:T(8,128)(2,1)S(1)} all-gather(bf16[1,1,576,128]{3,2,1,0:T(8,128)(2,1)} %param.14), channel_id=3, replica_groups=mesh['groups'=2,'seq'=4,'heads'=2,'cfg'=2] {'heads'}, dimensions={2}, use_global_device_ids=true | all-gather | bytes 442368 | tf_op jit(solution)/shard_map/all_gather | solution.py:55
  16.6 3.0 fusion.87
  19.6 28.1 %all-gather.12.cloned.1.call-done = bf16[1,1,1152,1024]{3,2,1,0:T(8,128)(2,1)} async-done(((bf16[1,1,576,1024]{3,2,1,0:T(8,128)(2,1)}), bf16[1,1,1152,1024]{3,2,1,0:T(8,128)(2,1)}) %all-gather.12.cloned.1.call-update) | async-done | bytes 2359312 | tf_op jit(solution)/shard_map/all_gather | solution.py:54
  47.7 2.3 fusion.50
  50.1 7.3 %fusion.48 = bf16[1,1024,3,576]{1,3,2,0:T(8,128)(2,1)S(1)} fusion(f32[1024]{0:T(1024)S(1)} %add_rsqrt_fusion.1, bf16[3,576,1152]{2,1,0:T(8,128)(2,1)} %param.19, bf16[1,1,1152,1024]{3,2,1,0:T(8,128)(2,1)S(1)} %copy-done.3, f32[1152]{0:T(1024)S(1)} %convert_element_type.98), kind=kOutput, calls=%fused_computation.28 | convolution fusion | flops 4083941376 | bytes 9888256 | tf_op jit(solution)/shard_map/kod,fdp->fkop/dot_general | solution.py:26
  60.1 37.0 %while.10 = (s32[]{:T(128)}, bf16[2,8,72,512]{3,2,1,0:T(8,128)(2,1)}, pred[1,1152]{1,0:T(4,128)(4,1)S(1)}, s32[2]{0:T(128)S(1)}, bf16[1,8,72,1024]{3,2,1,0:T(8,1...) while((s32[]{:T(128)}, ...), condition=%wide.region_5.6_spmd, body=%wide.region_2.5_spmd.sunk | while | flops 2081200384 | bytes 5788856 | solution.py:90
  61.9 7.0 %exponential_reduce_fusion.2 = f32[8,512]{1,0:T(8,128)S(1)} fusion(pred[1152]{0:T(1024)(128)(4,1)S(1)} %reduce.5, bf16[1,8,72,1152]{3,2,1,0:T(8,128)(2,1)S(1)} %get-tuple-element.139, bf16[1,8,72,1024]{3,2,1,0:T(8,128)(2,1)} %get-tuple-element.138, s32[]{:T(128)S(6)} %select_n.52), kind=kOutput, calls=%fused_computation.5.clone.1 | convolution fusion | flops 698352768 | bytes 1934468 | tf_op jit(solution)/shard_map/while/body/eval_jaxpr/sub | solution.py:17
  69.0 9.8 %fusion.120 = bf16[2,8,72,512]{3,2,1,0:T(8,128)(2,1)} fusion(bf16[2,8,72,512]{3,2,1,0:T(8,128)(2,1)} %get-tuple-element.123, s32[]{:T(128)} %get-tuple-element.122, bf16[1,8,72,1152]{3,2,1,0:T(8,128)(2,1)} %get-tuple-element.140, f32[8,512]{1,0:T(8,128)S(1)} %exponential_reduce_fusion.2, pred[1152]{0:T(1024)(128)(4,1)S(1)} %reduce.5, ...), kind=kOutput, calls=%fused_computation.13.clone.1 | convolution fusion | flops 1382847616 | bytes 3851908 | tf_op jit(solution)/shard_map/while/body/eval_jaxpr/hpk,hek->hep/dot_general | solution.py:85
  80.2 7.0 %exponential_reduce_fusion.2 = f32[8,512]{1,0:T(8,128)S(1)} fusion(pred[1152]{0:T(1024)(128)(4,1)S(1)} %reduce.5, bf16[1,8,72,1152]{3,2,1,0:T(8,128)(2,1)S(1)} %get-tuple-element.139, bf16[1,8,72,1024]{3,2,1,0:T(8,128)(2,1)} %get-tuple-element.138, s32[]{:T(128)S(6)} %select_n.52), kind=kOutput, calls=%fused_computation.5.clone.1 | convolution fusion | flops 698352768 | bytes 1934468 | tf_op jit(solution)/shard_map/while/body/eval_jaxpr/sub | solution.py:17
  87.2 9.8 %fusion.120 = bf16[2,8,72,512]{3,2,1,0:T(8,128)(2,1)} fusion(bf16[2,8,72,512]{3,2,1,0:T(8,128)(2,1)} %get-tuple-element.123, s32[]{:T(128)} %get-tuple-element.122, bf16[1,8,72,1152]{3,2,1,0:T(8,128)(2,1)} %get-tuple-element.140, f32[8,512]{1,0:T(8,128)S(1)} %exponential_reduce_fusion.2, pred[1152]{0:T(1024)(128)(4,1)S(1)} %reduce.5, ...), kind=kOutput, calls=%fused_computation.13.clone.1 | convolution fusion | flops 1382847616 | bytes 3851908 | tf_op jit(solution)/shard_map/while/body/eval_jaxpr/hpk,hek->hep/dot_general | solution.py:85
  97.1 2.5 copy.43
  101.5 36.0 %all-gather.8.cloned.1.call-done = bf16[1,1152,1024]{2,1,0:T(8,128)(2,1)} async-done(((bf16[1,576,1024]{2,1,0:T(8,128)(2,1)}), bf16[1,1152,1024]{2,1,0:T(8,128)(2,1)}) %all-gather.8.cloned.1.call-update) | async-done | bytes 2359312 | tf_op jit(solution)/shard_map/all_gather | solution.py:93
  137.5 3.7 %fusion.64 = bf16[1,576,1024]{2,1,0:T(8,128)(2,1)S(1)} fusion(bf16[576,1152]{1,0:T(8,128)(2,1)S(1)} %copy-done, bf16[1,1152,1024]{2,1,0:T(8,128)(2,1)} %all-gather.8.cloned.1.call-done, bf16[1,1,576,1024]{3,2,1,0:T(8,128)(2,1)} %param.13), kind=kOutput, calls=%fused_computation.47 | convolution fusion | flops 1360723968 | bytes 6045696 | tf_op jit(solution)/shard_map/oc,fcp->fop/dot_general | solution.py:31
  141.1 4.1 %copy.44 = bf16[1,576,1024]{1,0,2:T(2,128)(2,1)} copy(bf16[1,576,1024]{2,1,0:T(8,128)(2,1)S(1)} %fusion.64) | data formatting | bytes 2359296 | tf_op jit(solution)/shard_map/convert_element_type | solution.py:94
  145.8 9.9 %reduce.3 = bf16[1024,576]{1,0:T(8,128)(2,1)S(1)} reduce(bf16[1024,1,576]{2,1,0:T(2,128)(2,1)} %bitcast.189, bf16[]{:T(256)} %broadcast.82), dimensions={1}, to_apply=%bitcast.164.reduce_sub_computation | reduce | bytes 2359298
  155.7 2.6 reshape.124
  158.3 33.0 %all_to_all.36 = bf16[4,2,73728]{2,1,0:T(2,128)(2,1)S(1)} all-to-all(bf16[4,2,73728]{2,1,0:T(2,128)(2,1)} %reshape.124), channel_id=1, replica_groups=mesh['groups'=2,'seq'=4,'heads'=2,'cfg'=2] {'seq'}, dimensions={0} | all-to-all | bytes 2359296 | tf_op jit(solution)/shard_map/all_to_all | solution.py:95
  191.3 3.3 reshape.125
  198.3 34.1 %all-gather.14.cloned.1.call-done = bf16[4,1,1152,256]{3,2,0,1:T(8,128)(2,1)} async-done(((bf16[4,1,576,256]{3,2,0,1:T(8,128)(2,1)}), bf16[4,1,1152,256]{3,2,0,1:T(8,128)(2,1)}) %all-gather.14.cloned.1.call-update) | async-done | bytes 2359312 | tf_op jit(solution)/shard_map/all_gather | solution.py:99
  232.3 2.3 fusion.52
  234.7 7.2 %multiply_convert_fusion = bf16[4,256,3,576]{1,3,2,0:T(8,128)(2,1)S(1)} fusion(f32[4,256]{1,0:T(4,128)S(1)} %add_rsqrt_fusion, bf16[3,576,1152]{2,1,0:T(8,128)(2,1)} %param.22, bf16[4,1,1152,256]{3,2,0,1:T(8,128)(2,1)S(1)} %copy-done.4, f32[1152]{0:T(1024)S(1)} %convert_element_type.109), kind=kOutput, calls=%fused_computation.29 | convolution fusion | flops 4083941376 | bytes 9888256 | tf_op jit(solution)/shard_map/kod,fdp->fkop/dot_general | solution.py:26
  243.8 2.8 copy.59
  246.7 4.1 %copy.60 = bf16[4,1,8,72,256]{3,0,4,2,1:T(4,128)(2,1)} copy(bf16[4,1,8,72,256]{4,3,2,1,0:T(8,128)(2,1)} %get-tuple-element.59) | data formatting | bytes 2359296
  250.7 5.8 %fusion.71 = f32[8,256,4,4]{3,2,1,0:T(4,128)} fusion(bf16[4,1,8,72,256]{3,0,4,2,1:T(4,128)(2,1)} %copy.60, bf16[4,1,8,72,256]{3,0,4,2,1:T(4,128)(2,1)S(1)} %copy.59), kind=kOutput, calls=%fused_computation.54 | convolution fusion | flops 4718592 | bytes 2490368 | tf_op jit(solution)/shard_map/fhep,ghep->hfgp/dot_general | solution.py:108
  256.5 2.8 copy.50
  261.6 2.5 copy.58
  264.1 5.8 %convert_bitcast_fusion = bf16[4,8,72,256]{2,0,3,1:T(4,128)(2,1)} fusion(bf16[8,4,4,256]{2,1,3,0:T(4,128)(2,1)} %copy.51, bf16[4,1,8,72,256]{3,0,4,2,1:T(4,128)(2,1)} %copy.58), kind=kOutput, calls=%fused_computation.59 | convolution fusion | flops 5308416 | bytes 2424832 | tf_op jit(solution)/shard_map/hfgp,ghep->fhep/dot_general | solution.py:112
  269.9 4.2 %copy.52 = bf16[4,8,72,256]{3,2,1,0:T(8,128)(2,1)} copy(bf16[4,8,72,256]{2,0,3,1:T(4,128)(2,1)} %convert_bitcast_fusion) | data formatting | bytes 2359296 | tf_op jit(solution)/shard_map/convert_element_type | solution.py:115
  274.1 36.2 %all-gather.10.cloned.1.call-done = bf16[4,1152,256]{2,1,0:T(8,128)(2,1)} async-done(((bf16[4,576,256]{2,1,0:T(8,128)(2,1)}), bf16[4,1152,256]{2,1,0:T(8,128)(2,1)}) %all-gather.10.cloned.1.call-update) | async-done | bytes 2359312 | tf_op jit(solution)/shard_map/all_gather | solution.py:117
  310.3 3.8 %fusion.63 = bf16[4,576,256]{2,1,0:T(8,128)(2,1)S(1)} fusion(bf16[4,1152,256]{2,1,0:T(8,128)(2,1)} %all-gather.10.cloned.1.call-done, bf16[576,1152]{1,0:T(8,128)(2,1)} %param.23, bf16[1,576,4,256]{3,1,2,0:T(8,128)(2,1)S(1)} %copy-done.2), kind=kOutput, calls=%fused_computation.45 | convolution fusion | flops 1360723968 | bytes 6045696 | tf_op jit(solution)/shard_map/oc,fcp->fop/dot_general | solution.py:31
  314.1 32.8 %all_to_all.37 = bf16[4,576,256]{2,1,0:T(8,128)(2,1)S(1)} all-to-all(bf16[4,576,256]{2,1,0:T(8,128)(2,1)S(1)} %fusion.63), channel_id=1, replica_groups=mesh['groups'=2,'seq'=4,'heads'=2,'cfg'=2] {'seq'}, dimensions={0} | all-to-all | bytes 2359296 | tf_op jit(solution)/shard_map/all_to_all | solution.py:120
  350.0 2.2 fusion.91
  (49 shorter events, 17.9 us)
Async XLA Ops:
  6.5 130.9 %copy-start = (bf16[576,1152]{1,0:T(8,128)(2,1)S(1)}, bf16[576,1152]{1,0:T(8,128)(2,1)}, u32[]{:S(2)}) copy-start(bf16[576,1152]{1,0:T(8,128)(2,1)} %param.20) | copy-start | bytes 3981316
  6.5 41.1 %all-gather.12.cloned.1.call-start = ((), (), s32[]{:S(2)}) async-start(), calls=%async_computation.4 | async-start | bytes 3538944 | tf_op jit(solution)/shard_map/all_gather | solution.py:54
  7.3 130.2 %all-gather.8.cloned.1.call-start = ((), (), s32[]{:S(2)}) async-start(), calls=%async_computation.2 | async-start | bytes 3538944 | tf_op jit(solution)/shard_map/all_gather | solution.py:93
  47.7 2.4 copy-start.3
  101.3 131.0 %all-gather.14.cloned.1.call-start = ((), (), s32[]{:S(2)}) async-start(), calls=%async_computation.5 | async-start | bytes 3538944 | tf_op jit(solution)/shard_map/all_gather | solution.py:99
  196.5 1.8 copy-start.5
  198.0 112.3 %all-gather.10.cloned.1.call-start = ((), (), s32[]{:S(2)}) async-start(), calls=%async_computation.3 | async-start | bytes 3538944 | tf_op jit(solution)/shard_map/all_gather | solution.py:117
  232.3 2.4 copy-start.4
  259.4 2.2 copy-start.1
  269.9 40.4 %copy-start.2 = (bf16[1,576,4,256]{3,1,2,0:T(8,128)(2,1)S(1)}, bf16[1,576,4,256]{3,1,2,0:T(8,128)(2,1)}, u32[]{:S(2)}) copy-start(bf16[1,576,4,256]{3,1,2,0:T(8,128)(2,1)} %copy.46) | copy-start | bytes 3538948
  347.0 3.0 collective-permute-start
Sparse Core Ops, SparseCore 0:
  8.9 38.7 all-gather.11
  101.4 36.0 all-gather.7
  198.1 34.1 all-gather.13
  274.2 36.0 all-gather.9
where the time goes:
time: 364 us; the launch traced here: 359 us
  waiting for transfers between devices  137 us (38%)
  blocking collectives  73.5 us (20%)
  matrix products  70.3 us (19%)
  local copies, waits for them, and re-layouts  41.4 us (11%)
  other arithmetic  19.1 us (5%)
  between operations  15.5 us (4%)
    all_gather x1, waiting for transfers between devices, shards(): lax.all_gather(attended_time, 'heads', axis=1, tiled=True)  36.2 us
    all_gather x1, waiting for transfers between devices, shards(): lax.all_gather(attended, 'heads', axis=1, tiled=True)  36 us
    all_gather x1, waiting for transfers between devices, shards(): lax.all_gather(own_rows, 'heads', axis=1, tiled=True)  34.1 us
    all_to_all x1, blocking collectives, shards(): lax.all_to_all(after_spatial, 'seq', split_axis=2, concat_axis=0, tiled=T...  33 us
    all_to_all x1, blocking collectives, shards(): lax.all_to_all(block_out, 'seq', split_axis=0, concat_axis=2, tiled=True)  32.8 us
    all_gather x1, waiting for transfers between devices, shards(): video_piece = lax.all_gather(frame_tokens, 'heads', axis=1, tiled=True)  28.1 us
    dot_general x2, matrix products, block_step(): jnp.einsum('hpk,hek->hep', weights, value_rows[frame_id], preferred_eleme...  19.7 us
    unnamed x19, local copies, waits for them, and re-layouts  17.8 us
  transfers between devices with their start and end apart: 5, of which 5 were waited for; matrix products, arithmetic and copies ran while one was open for 1% of the time, Pallas kernels for 0%

commit v1 on v0

--- a/solution.py
+++ b/solution.py
@@ -6,6 +6,15 @@
 D = 1152
 HEAD_DIM = 72
 epsilon = 1e-06
+pairs_all_match = lambda block_in, on_dim, join_dim: jnp.concatenate(
+    jax.lax.all_to_all(
+        jnp.stack(jnp.split(block_in, jax.lax.axis_size("seq"), axis=on_dim), axis=0),
+        axis_name="seq",
+        concat_axis=0,
+        split_axis=0,
+    ),
+    axis=join_dim,
+)
 
 
 def from_partner(shard, axis, stride):
@@ -92,7 +101,7 @@
     attended = jnp.transpose(attended, (0, 2, 3, 1, 4)).reshape(frame_count, width, positions)
     update = add_mixed(lax.all_gather(attended, "heads", axis=1, tiled=True), spatial_out)
     after_spatial = (frame_tokens.astype(jnp.float32) + update).astype(jnp.bfloat16)
-    own_rows = lax.all_to_all(after_spatial, "seq", split_axis=2, concat_axis=0, tiled=True)
+    own_rows = pairs_all_match(after_spatial, on_dim=2, join_dim=0)
     frames_all = own_rows.shape[0]
     columns = own_rows.shape[2]
     piece_add, piece_sq = project_piece(

time: 364 us -> 335 us (0.920); the launches traced: 359 us -> 335 us
  local copies, waits for them, and re-layouts: 41.4 us -> 27.6 us
  other arithmetic: 19.1 us -> 9.33 us
    unnamed x1 -> x0, other arithmetic: 9.93 us -> none
    unnamed x19 -> x15, local copies, waits for them, and re-layouts: 17.8 us -> 9.5 us
    convert_element_type x1 -> x0, local copies, waits for them, and re-layouts: 4.11 us -> none  [shards(): (frame_tokens.astype(jnp.float32) + update).astype(jnp.bfloat16)]
where the time goes in v1:
time: 335 us
  waiting for transfers between devices  137 us (41%)
  blocking collectives  73.4 us (22%)
  matrix products  70.3 us (21%)
  local copies, waits for them, and re-layouts  27.6 us (8%)
  between operations  15.3 us (5%)
  other arithmetic  9.33 us (3%)
    all_gather x1, waiting for transfers between devices, shards(): lax.all_gather(attended_time, 'heads', axis=1, tiled=True)  36.2 us
    all_gather x1, waiting for transfers between devices, shards(): lax.all_gather(attended, 'heads', axis=1, tiled=True)  35.9 us
    all_gather x1, waiting for transfers between devices, shards(): lax.all_gather(own_rows, 'heads', axis=1, tiled=True)  34.3 us
    all_to_all x1, blocking collectives, jax.lax.all_to_all(jnp.stack(jnp.split(block_in, jax.lax.axis_size('seq')...  32.9 us
    all_to_all x1, blocking collectives, shards(): lax.all_to_all(block_out, 'seq', split_axis=0, concat_axis=2, tiled=True)  32.8 us
    all_gather x1, waiting for transfers between devices, shards(): video_piece = lax.all_gather(frame_tokens, 'heads', axis=1, tiled=True)  28.1 us
    dot_general x2, matrix products, block_step(): jnp.einsum('hpk,hek->hep', weights, value_rows[frame_id], preferred_eleme...  19.7 us
    dot_general x3, matrix products, project_piece(): jnp.einsum('kod,fdp->fkop', weight_piece, scaled, preferred_element_type=...  17.5 us
  transfers between devices with their start and end apart: 5, of which 5 were waited for; matrix products, arithmetic and copies ran while one was open for 1% of the time, Pallas kernels for 0%

profile of v1, /device:TPU:0, one launch (start us, length us, event | category | flops | bytes accessed | tf_op | source)
XLA Modules:
  0.0 334.6 jit_solution(12909776162323412480)
XLA Ops:
  8.7 7.7 %all-gather.1 = bf16[1,1,1152,128]{3,2,1,0:T(8,128)(2,1)S(1)} all-gather(bf16[1,1,576,128]{3,2,1,0:T(8,128)(2,1)} %param.14), channel_id=3, replica_groups=mesh['groups'=2,'seq'=4,'heads'=2,'cfg'=2] {'heads'}, dimensions={2}, use_global_device_ids=true | all-gather | bytes 442368 | tf_op jit(solution)/shard_map/all_gather | solution.py:64
  16.6 3.0 fusion.87
  19.6 28.1 %all-gather.12.cloned.1.call-done = bf16[1,1,1152,1024]{3,2,1,0:T(8,128)(2,1)} async-done(((bf16[1,1,576,1024]{3,2,1,0:T(8,128)(2,1)}), bf16[1,1,1152,1024]{3,2,1,0:T(8,128)(2,1)}) %all-gather.12.cloned.1.call-update) | async-done | bytes 2359312 | tf_op jit(solution)/shard_map/all_gather | solution.py:63
  47.7 2.3 fusion.50
  50.1 7.3 %fusion.48 = bf16[1,1024,3,576]{1,3,2,0:T(8,128)(2,1)S(1)} fusion(f32[1024]{0:T(1024)S(1)} %add_rsqrt_fusion.1, bf16[3,576,1152]{2,1,0:T(8,128)(2,1)} %param.19, bf16[1,1,1152,1024]{3,2,1,0:T(8,128)(2,1)S(1)} %copy-done.3, f32[1152]{0:T(1024)S(1)} %convert_element_type.98), kind=kOutput, calls=%fused_computation.28 | convolution fusion | flops 4083941376 | bytes 9888256 | tf_op jit(solution)/shard_map/kod,fdp->fkop/dot_general | solution.py:35
  60.1 36.6 %while.10 = (s32[]{:T(128)}, bf16[2,8,72,512]{3,2,1,0:T(8,128)(2,1)}, pred[1,1152]{1,0:T(4,128)(4,1)S(1)}, s32[2]{0:T(128)S(1)}, bf16[1,8,72,1024]{3,2,1,0:T(8,1...) while((s32[]{:T(128)}, ...), condition=%wide.region_5.6_spmd, body=%wide.region_2.5_spmd.sunk | while | flops 2081200384 | bytes 5788856 | solution.py:99
  61.5 7.0 %exponential_reduce_fusion.2 = f32[8,512]{1,0:T(8,128)S(1)} fusion(pred[1152]{0:T(1024)(128)(4,1)S(1)} %reduce.4, bf16[1,8,72,1152]{3,2,1,0:T(8,128)(2,1)S(1)} %get-tuple-element.143, bf16[1,8,72,1024]{3,2,1,0:T(8,128)(2,1)} %get-tuple-element.142, s32[]{:T(128)S(6)} %select_n.52), kind=kOutput, calls=%fused_computation.5.clone.1 | convolution fusion | flops 698352768 | bytes 1934468 | tf_op jit(solution)/shard_map/while/body/eval_jaxpr/sub | solution.py:26
  68.5 9.8 %fusion.120 = bf16[2,8,72,512]{3,2,1,0:T(8,128)(2,1)} fusion(bf16[2,8,72,512]{3,2,1,0:T(8,128)(2,1)} %get-tuple-element.127, s32[]{:T(128)} %get-tuple-element.126, bf16[1,8,72,1152]{3,2,1,0:T(8,128)(2,1)} %get-tuple-element.144, f32[8,512]{1,0:T(8,128)S(1)} %exponential_reduce_fusion.2, pred[1152]{0:T(1024)(128)(4,1)S(1)} %reduce.4, ...), kind=kOutput, calls=%fused_computation.13.clone.1 | convolution fusion | flops 1382847616 | bytes 3851908 | tf_op jit(solution)/shard_map/while/body/eval_jaxpr/hpk,hek->hep/dot_general | solution.py:94
  79.8 7.0 %exponential_reduce_fusion.2 = f32[8,512]{1,0:T(8,128)S(1)} fusion(pred[1152]{0:T(1024)(128)(4,1)S(1)} %reduce.4, bf16[1,8,72,1152]{3,2,1,0:T(8,128)(2,1)S(1)} %get-tuple-element.143, bf16[1,8,72,1024]{3,2,1,0:T(8,128)(2,1)} %get-tuple-element.142, s32[]{:T(128)S(6)} %select_n.52), kind=kOutput, calls=%fused_computation.5.clone.1 | convolution fusion | flops 698352768 | bytes 1934468 | tf_op jit(solution)/shard_map/while/body/eval_jaxpr/sub | solution.py:26
  86.8 9.8 %fusion.120 = bf16[2,8,72,512]{3,2,1,0:T(8,128)(2,1)} fusion(bf16[2,8,72,512]{3,2,1,0:T(8,128)(2,1)} %get-tuple-element.127, s32[]{:T(128)} %get-tuple-element.126, bf16[1,8,72,1152]{3,2,1,0:T(8,128)(2,1)} %get-tuple-element.144, f32[8,512]{1,0:T(8,128)S(1)} %exponential_reduce_fusion.2, pred[1152]{0:T(1024)(128)(4,1)S(1)} %reduce.4, ...), kind=kOutput, calls=%fused_computation.13.clone.1 | convolution fusion | flops 1382847616 | bytes 3851908 | tf_op jit(solution)/shard_map/while/body/eval_jaxpr/hpk,hek->hep/dot_general | solution.py:94
  96.6 2.5 copy.23
  99.1 1.7 reshape.108
  101.1 35.9 %all-gather.8.cloned.1.call-done = bf16[1,1152,1024]{2,1,0:T(8,128)(2,1)} async-done(((bf16[1,576,1024]{2,1,0:T(8,128)(2,1)}), bf16[1,1152,1024]{2,1,0:T(8,128)(2,1)}) %all-gather.8.cloned.1.call-update) | async-done | bytes 2359312 | tf_op jit(solution)/shard_map/all_gather | solution.py:102
  137.0 3.7 %fusion.64 = bf16[1,576,1024]{2,1,0:T(8,128)(2,1)S(1)} fusion(bf16[576,1152]{1,0:T(8,128)(2,1)S(1)} %copy-done, bf16[1,1152,1024]{2,1,0:T(8,128)(2,1)} %all-gather.8.cloned.1.call-done, bf16[1,1,576,1024]{3,2,1,0:T(8,128)(2,1)} %param.13), kind=kOutput, calls=%fused_computation.47 | convolution fusion | flops 1360723968 | bytes 6045696 | tf_op jit(solution)/shard_map/oc,fcp->fop/dot_general | solution.py:40
  140.9 32.9 %all_to_all.23 = bf16[4,1,576,256]{3,2,1,0:T(8,128)(2,1)} all-to-all(bf16[4,1,576,256]{3,2,1,0:T(8,128)(2,1)S(1)} %pad_maximum_fusion.2), channel_id=1, replica_groups=mesh['groups'=2,'seq'=4,'heads'=2,'cfg'=2] {'seq'}, dimensions={0} | all-to-all | bytes 2359296 | tf_op jit(solution)/shard_map/all_to_all | solution.py:10
  173.9 34.3 %all-gather.14.cloned.1.call-done = bf16[4,1,1152,256]{3,2,1,0:T(8,128)(2,1)} async-done(((bf16[4,1,576,256]{3,2,1,0:T(8,128)(2,1)}), bf16[4,1,1152,256]{3,2,1,0:T(8,128)(2,1)}) %all-gather.14.cloned.1.call-update) | async-done | bytes 2359312 | tf_op jit(solution)/shard_map/all_gather | solution.py:108
  208.2 2.3 fusion.52
  210.6 7.2 %multiply_convert_fusion = bf16[4,256,3,576]{1,3,2,0:T(8,128)(2,1)S(1)} fusion(f32[4,256]{1,0:T(4,128)S(1)} %add_rsqrt_fusion, bf16[3,576,1152]{2,1,0:T(8,128)(2,1)} %param.22, bf16[4,1,1152,256]{3,2,1,0:T(8,128)(2,1)S(1)} %copy-done.4, f32[1152]{0:T(1024)S(1)} %convert_element_type.109), kind=kOutput, calls=%fused_computation.29 | convolution fusion | flops 4083941376 | bytes 9888256 | tf_op jit(solution)/shard_map/kod,fdp->fkop/dot_general | solution.py:35
  217.8 1.9 fusion.104
  219.7 2.8 copy.33
  222.5 4.1 %copy.34 = bf16[4,1,8,72,256]{3,0,4,2,1:T(4,128)(2,1)} copy(bf16[4,1,8,72,256]{4,3,2,1,0:T(8,128)(2,1)} %get-tuple-element.59) | data formatting | bytes 2359296
  226.6 5.8 %fusion.71 = f32[8,256,4,4]{3,2,1,0:T(4,128)} fusion(bf16[4,1,8,72,256]{3,0,4,2,1:T(4,128)(2,1)} %copy.34, bf16[4,1,8,72,256]{3,0,4,2,1:T(4,128)(2,1)S(1)} %copy.33), kind=kOutput, calls=%fused_computation.54 | convolution fusion | flops 4718592 | bytes 2490368 | tf_op jit(solution)/shard_map/fhep,ghep->hfgp/dot_general | solution.py:117
  232.4 2.8 copy.27
  235.4 2.1 copy.28
  237.5 2.5 copy.32
  240.0 5.8 %convert_bitcast_fusion = bf16[4,8,72,256]{2,0,3,1:T(4,128)(2,1)} fusion(bf16[8,4,4,256]{2,1,3,0:T(4,128)(2,1)} %copy.28, bf16[4,1,8,72,256]{3,0,4,2,1:T(4,128)(2,1)} %copy.32), kind=kOutput, calls=%fused_computation.59 | convolution fusion | flops 5308416 | bytes 2424832 | tf_op jit(solution)/shard_map/hfgp,ghep->fhep/dot_general | solution.py:121
  245.8 4.2 %copy.29 = bf16[4,8,72,256]{3,2,1,0:T(8,128)(2,1)} copy(bf16[4,8,72,256]{2,0,3,1:T(4,128)(2,1)} %convert_bitcast_fusion) | data formatting | bytes 2359296 | tf_op jit(solution)/shard_map/convert_element_type | solution.py:124
  250.0 36.2 %all-gather.10.cloned.1.call-done = bf16[4,1152,256]{2,1,0:T(8,128)(2,1)} async-done(((bf16[4,576,256]{2,1,0:T(8,128)(2,1)}), bf16[4,1152,256]{2,1,0:T(8,128)(2,1)}) %all-gather.10.cloned.1.call-update) | async-done | bytes 2359312 | tf_op jit(solution)/shard_map/all_gather | solution.py:126
  286.2 3.8 %fusion.63 = bf16[4,576,256]{2,1,0:T(8,128)(2,1)S(1)} fusion(bf16[4,1152,256]{2,1,0:T(8,128)(2,1)} %all-gather.10.cloned.1.call-done, bf16[576,1152]{1,0:T(8,128)(2,1)} %param.23, bf16[4,1,576,256]{3,2,1,0:T(8,128)(2,1)S(1)} %copy-done.2), kind=kOutput, calls=%fused_computation.45 | convolution fusion | flops 1360723968 | bytes 6045696 | tf_op jit(solution)/shard_map/oc,fcp->fop/dot_general | solution.py:40
  290.0 32.8 %all_to_all.24 = bf16[4,576,256]{2,1,0:T(8,128)(2,1)S(1)} all-to-all(bf16[4,576,256]{2,1,0:T(8,128)(2,1)S(1)} %fusion.63), channel_id=1, replica_groups=mesh['groups'=2,'seq'=4,'heads'=2,'cfg'=2] {'seq'}, dimensions={0} | all-to-all | bytes 2359296 | tf_op jit(solution)/shard_map/all_to_all | solution.py:129
  324.3 1.6 collective-permute-done
  325.9 2.2 fusion.91
  (44 shorter events, 6.8 us)
Async XLA Ops:
  6.5 130.5 %copy-start = (bf16[576,1152]{1,0:T(8,128)(2,1)S(1)}, bf16[576,1152]{1,0:T(8,128)(2,1)}, u32[]{:S(2)}) copy-start(bf16[576,1152]{1,0:T(8,128)(2,1)} %param.20) | copy-start | bytes 3981316
  6.5 41.1 %all-gather.12.cloned.1.call-start = ((), (), s32[]{:S(2)}) async-start(), calls=%async_computation.4 | async-start | bytes 3538944 | tf_op jit(solution)/shard_map/all_gather | solution.py:63
  7.3 129.8 %all-gather.8.cloned.1.call-start = ((), (), s32[]{:S(2)}) async-start(), calls=%async_computation.2 | async-start | bytes 3538944 | tf_op jit(solution)/shard_map/all_gather | solution.py:102
  47.7 2.4 copy-start.3
  100.8 107.4 %all-gather.14.cloned.1.call-start = ((), (), s32[]{:S(2)}) async-start(), calls=%async_computation.5 | async-start | bytes 3538944 | tf_op jit(solution)/shard_map/all_gather | solution.py:108
  140.9 33.0 %copy-start.5 = (bf16[1152]{0:T(1024)(128)(2,1)S(1)}, bf16[1152]{0:T(1024)(128)(2,1)}, u32[]{:S(2)}) copy-start(bf16[1152]{0:T(1024)(128)(2,1)} %param.21) | copy-start | bytes 6916
  173.8 112.3 %all-gather.10.cloned.1.call-start = ((), (), s32[]{:S(2)}) async-start(), calls=%async_computation.3 | async-start | bytes 3538944 | tf_op jit(solution)/shard_map/all_gather | solution.py:126
  208.2 2.4 copy-start.4
  235.3 2.2 copy-start.1
  245.8 40.4 %copy-start.2 = (bf16[4,1,576,256]{3,2,1,0:T(8,128)(2,1)S(1)}, bf16[4,1,576,256]{3,2,1,0:T(8,128)(2,1)}, u32[]{:S(2)}) copy-start(bf16[4,1,576,256]{3,2,1,0:T(8,128)(2,1)} %all_to_all.23) | copy-start | bytes 3538948
  322.9 3.0 collective-permute-start
Sparse Core Ops, SparseCore 0:
  8.9 38.7 all-gather.11
  100.9 36.0 all-gather.7
  174.0 34.1 all-gather.13
  250.1 36.0 all-gather.9
